TPU v7x, 32 devices: a whole 2x2x4 slice. The times are simulated.
32 devices in a mesh: groups: 2 (over y), seq: 4 (over z), tp: 4 (over x, core).
Axes of the slice: x: 2, y: 2, z: 4, core: 2. Of those that a mesh axis runs over, the one named last changes fastest.
Arguments:
- prompt_kv: bfloat16 [32768, 64, 128], P(('groups', 'seq', 'tp')), parts along dimension 0, may hold values from -6 to 6
- prompt_length: int32 [2], P('groups'), parts along dimension 0, may hold values from 8192 to 16384
- queries: bfloat16 [16, 4096], P('groups'), parts along dimension 0, may hold values from -6 to 6
- new_kv: bfloat16 [16, 16, 2, 128], P('groups'), parts along dimension 0, may hold values from -6 to 6
- k_cache: bfloat16 [256, 8192, 128], P(('groups', 'seq'), 'tp'), parts along dimension 0, may hold values from -6 to 6
- v_cache: bfloat16 [256, 8192, 128], P(('groups', 'seq'), 'tp'), parts along dimension 0, may hold values from -6 to 6
- lengths: int32 [16], P('groups'), parts along dimension 0, may hold values from 4097 to 8192
- slots: int32 [16], P('groups'), parts along dimension 0, may hold values from 0 to 7, each once
Outputs:
- prompt_owned: bfloat16 [32768, 64, 128], P(('groups', 'tp'), 'seq'), parts along dimension 0
- attended: bfloat16 [256, 256], P(('groups', 'seq')), parts along dimension 0
There are 2 independent parts, one for each index of `groups`. A program takes and returns all parts, laid end to end along the dimension named above; each array names one. Nothing has to cross between parts.
Inputs may be any that keep to these rules, and one draw needn't show every extreme that they name: `slots`: each slot once.
All inputs are finite; a program needn't handle non-finite values.
Results may differ from a plain program's by a relative error of at most 0.0028.
Values may be sent and summed in bfloat16 or wider, within the bound.
No kernel may reach another device: no remote copies, remote signals or barrier semaphores. Data moves between devices by JAX's collectives and lax.ppermute only.
A program may use at most 128 MiB of HBM per device.

v0:
```python
import jax
import jax.numpy as jnp
from jax import lax
from jax.sharding import PartitionSpec as P

query_scale = 168.0 ** (-0.5)
negative = -1e30


def merged(part, axis, combine):
    gathered = jax.tree.map(lambda a: lax.all_gather(a, axis), part)

    def take(source):
        return jax.tree.map(lambda a: lax.dynamic_index_in_dim(a, source, 0, False), gathered)

    return lax.fori_loop(
        1, lax.axis_size(axis), lambda source, state: combine(state, take(source)), take(0)
    )


def combine_parts(first, second):
    upper = jnp.maximum(first[0], second[0])
    scale_one = jnp.exp(first[0] - upper)
    scale_two = jnp.exp(second[0] - upper)
    total = first[1] * scale_one + second[1] * scale_two
    summed = first[2] * scale_one[..., None] + second[2] * scale_two[..., None]
    return (upper, total, summed)


def per_device(prompt_kv, prompt_length, queries, new_kv, k_cache, v_cache, lengths, slots):
    block = prompt_kv.shape[0]
    offset = (lax.axis_index("seq") * lax.axis_size("tp") + lax.axis_index("tp")) * block
    position = offset + jnp.arange(block, dtype=jnp.int32)
    kept = jnp.where(
        (position < prompt_length[0])[:, None, None], prompt_kv, jnp.zeros_like(prompt_kv)
    )
    prompt_owned = lax.all_to_all(kept, "seq", split_axis=1, concat_axis=0, tiled=True)
    resident = lengths.shape[0]
    pair_rows = k_cache.shape[0]
    span = k_cache.shape[1]
    width = k_cache.shape[2]
    heads = new_kv.shape[1]
    group = queries.shape[1] // (heads * width)
    rows = lax.axis_index("seq") * pair_rows + jnp.arange(pair_rows, dtype=jnp.int32)
    head_of = rows // resident
    slot_of = rows % resident
    match = slots[None, :] == slot_of[:, None]
    sequence = jnp.sum(jnp.where(match, jnp.arange(resident, dtype=jnp.int32)[None, :], 0), axis=1)
    grouped = queries.reshape(resident, heads, group, width)
    query_rows = grouped[sequence, head_of]
    own = new_kv[sequence, head_of]
    own_key = own[:, 0]
    own_value = own[:, 1].astype(jnp.float32)
    live_len = lengths[sequence]
    scores = (
        jnp.einsum("rgd,rpd->rgp", query_rows, k_cache, preferred_element_type=jnp.float32)
        * query_scale
    )
    own_score = (
        jnp.einsum("rgd,rd->rg", query_rows, own_key, preferred_element_type=jnp.float32)
        * query_scale
    )
    cache_pos = lax.axis_index("tp") * span + jnp.arange(span, dtype=jnp.int32)
    live = cache_pos[None, None, :] < live_len[:, None, None]
    masked = jnp.where(live, scores, negative)
    local_top = jnp.max(masked, axis=2)
    weights = jnp.where(live, jnp.exp(masked - local_top[..., None]), 0.0)
    partial_value = jnp.einsum(
        "rgp,rpd->rgd", weights.astype(jnp.bfloat16), v_cache, preferred_element_type=jnp.float32
    )
    upper, total, summed = merged(
        (local_top, jnp.sum(weights, axis=2), partial_value), "tp", combine_parts
    )
    overall = jnp.maximum(upper, own_score)
    rescale = jnp.exp(upper - overall)
    own_weight = jnp.exp(own_score - overall)
    total = total * rescale + own_weight
    summed = summed * rescale[..., None] + own_weight[..., None] * own_value[:, None, :]
    attended = (summed / total[..., None]).astype(jnp.bfloat16).reshape(pair_rows, group * width)
    return (prompt_owned, attended)


def solution(mesh):
    in_specs = (
        P(("groups", "seq", "tp"), None, None),
        P("groups"),
        P("groups", None),
        P("groups", None, None, None),
        P(("groups", "seq"), "tp", None),
        P(("groups", "seq"), "tp", None),
        P("groups"),
        P("groups"),
    )
    out_specs = (P(("groups", "tp"), "seq", None), P(("groups", "seq"), None))
    return jax.shard_map(
        per_device, mesh=mesh, in_specs=in_specs, out_specs=out_specs, check_vma=False
    )
```

profile of v0, /device:TPU:0, one launch (start us, length us, event | category | flops | bytes accessed | tf_op | source)
XLA Modules:
  0.0 412.0 jit_solution(3879226195800347556)
XLA Ops:
  1.3 20.4 %copy_select_fusion = bf16[1024,64,128]{2,0,1:T(8,128)(2,1)} fusion(bf16[1024,64,128]{2,1,0:T(8,128)(2,1)} %param.10, pred[1024]{0:T(1024)(128)(4,1)S(1)} %add_compare_fusion), kind=kLoop, calls=%fused_computation.12 | loop fusion | flops 8388608 | bytes 33555456 | tf_op jit(solution)/shard_map/jit(_where)/select_n | solution.py:34
  21.7 7.1 %all-to-all-start = ((bf16[1024,64,128]{2,0,1:T(8,128)(2,1)}), bf16[1024,64,128]{2,0,1:T(8,128)(2,1)}, u32[]{:S(2)}, u32[]{:S(2)}) async-start(bf16[1024,64,128]{2,0,1:T(8,128)(2,1)} %copy_select_fusion), calls=%async_computation | async-start | bytes 33554432 | tf_op jit(solution)/shard_map/all_to_all | solution.py:37
  29.1 0.7 gather_fusion.1
  29.7 0.7 gather_fusion
  30.4 0.1 broadcast_compare_fusion
  30.5 10.3 %fusion.21 = (f32[32,2]{1,0:T(8,128)S(1)}, f32[32,2,2048]{2,1,0:T(2,128)S(1)}) fusion(bf16[32,2,128]{2,1,0:T(2,128)(2,1)S(1)} %gather_fusion.1, bf16[32,2048,128]{2,1,0:T(8,128)(2,1)} %param.14, pred[32,2048]{1,0:T(8,128)(4,1)S(1)} %broadcast_compare_fusion), kind=kOutput, calls=%fused_computation.54 | convolution fusion | flops 33947584 | bytes 17383680 | tf_op jit(solution)/shard_map/rgd,rpd->rgp/dot_general | solution.py:56
  40.9 0.7 fusion.6
  41.7 7.1 %fusion.4 = f32[32,2,128]{2,1,0:T(2,128)S(1)} fusion(bf16[32,2048,128]{2,1,0:T(8,128)(2,1)} %param.15, f32[32,2,2048]{2,1,0:T(2,128)S(1)} %get-tuple-element.207, pred[32,2048]{1,0:T(8,128)(4,1)S(1)} %broadcast_compare_fusion, f32[32,2]{1,0:T(8,128)S(1)} %get-tuple-element.206), kind=kOutput, calls=%fused_computation.16 | convolution fusion | flops 33947648 | bytes 17400064 | tf_op jit(solution)/shard_map/rgp,rpd->rgd/dot_general | solution.py:68
  48.8 6.5 %all-gather.2 = f32[128,2,128]{2,1,0:T(2,128)S(1)} all-gather(f32[32,2,128]{2,1,0:T(2,128)S(1)} %fusion.4), channel_id=4, replica_groups=mesh['groups'=2,'seq'=4,'tp'=4] {'tp'}, dimensions={0}, use_global_device_ids=true | all-gather | bytes 163840 | tf_op jit(solution)/shard_map/all_gather | solution.py:11
  55.3 0.7 gather_fusion.2
  56.0 0.1 fusion.8
  56.2 5.2 %all-gather.3 = f32[4,32,2]{1,2,0:T(2,128)S(1)} all-gather(f32[1,32,2]{1,2,0:T(2,128)S(1)} %bitcast.67), channel_id=2, replica_groups=mesh['groups'=2,'seq'=4,'tp'=4] {'tp'}, dimensions={0}, use_global_device_ids=true | all-gather | bytes 1280 | tf_op jit(solution)/shard_map/all_gather | solution.py:11
  61.5 5.1 %all-gather.4 = f32[4,32,2]{1,2,0:T(2,128)S(1)} all-gather(f32[1,32,2]{1,2,0:T(2,128)S(1)} %bitcast.68), channel_id=3, replica_groups=mesh['groups'=2,'seq'=4,'tp'=4] {'tp'}, dimensions={0}, use_global_device_ids=true | all-gather | bytes 1280 | tf_op jit(solution)/shard_map/all_gather | solution.py:11
  66.5 1.3 while.19
  66.5 0.1 copy.57
  66.7 0.2 fusion.29
  67.2 0.2 fusion.29
  67.5 0.1 copy.58
  67.6 0.2 fusion.29
  67.9 0.1 copy.48
  68.2 0.2 fusion.7
  68.3 0.6 copy.54
  69.0 324.5 %all-to-all-done = bf16[1024,64,128]{2,0,1:T(8,128)(2,1)} async-done(((bf16[1024,64,128]{2,0,1:T(8,128)(2,1)}), bf16[1024,64,128]{2,0,1:T(8,128)(2,1)}, u32[]{:S(2)}, u32[]{:S(2)}) %all-to-all-start) | async-done | bytes 16777248 | tf_op jit(solution)/shard_map/all_to_all | solution.py:37
  393.4 18.6 %copy.43 = bf16[4,1024,16,128]{3,2,1,0:T(8,128)(2,1)} copy(bf16[4,1024,16,128]{3,1,2,0:T(8,128)(2,1)} %bitcast.5) | data formatting | bytes 33554432 | tf_op jit(solution)/shard_map/all_to_all | solution.py:37
  (32 shorter events, 1.1 us)
Async XLA Ops:
  0.6 54.7 %copy-start = (bf16[8,16,2,128]{3,2,1,0:T(2,128)(2,1)S(1)}, bf16[8,16,2,128]{3,2,1,0:T(2,128)(2,1)}, u32[]{:S(2)}) copy-start(bf16[8,16,2,128]{3,2,1,0:T(2,128)(2,1)} %param.13) | copy-start | bytes 196612
  21.7 7.1 %copy-start.2 = (bf16[8,4096]{1,0:T(8,128)(2,1)S(1)}, bf16[8,4096]{1,0:T(8,128)(2,1)}, u32[]{:S(2)}) copy-start(bf16[8,4096]{1,0:T(8,128)(2,1)} %param.12) | copy-start | bytes 196612
  21.7 7.2 %copy-start.3 = (s32[8]{0:T(128)S(1)}, s32[8]{0:T(128)}, u32[]{:S(2)}) copy-start(s32[8]{0:T(128)} %param.17) | copy-start | bytes 100
  21.7 8.0 %copy-start.1 = (s32[8]{0:T(128)S(1)}, s32[8]{0:T(128)}, u32[]{:S(2)}) copy-start(s32[8]{0:T(128)} %param.16) | copy-start | bytes 100
  21.7 371.7 %all-to-all-start = ((bf16[1024,64,128]{2,0,1:T(8,128)(2,1)}), bf16[1024,64,128]{2,0,1:T(8,128)(2,1)}, u32[]{:S(2)}, u32[]{:S(2)}) async-start(bf16[1024,64,128]{2,0,1:T(8,128)(2,1)} %copy_select_fusion), calls=%async_computation | async-start | bytes 33554432 | tf_op jit(solution)/shard_map/all_to_all | solution.py:37
where the time goes:
time: 413 us; the launch traced here: 412 us
  waiting for transfers between devices  324 us (78%)
  local copies, waits for them, and re-layouts  22.3 us (5%)
  other arithmetic  22.3 us (5%)
  matrix products  17.5 us (4%)
  blocking collectives  16.8 us (4%)
  starting transfers between devices  7.11 us (2%)
    all_to_all x1, waiting for transfers between devices, per_device(): lax.all_to_all(kept, 'seq', split_axis=1, concat_axis=0, tiled=True)  324 us
    select_n x1, other arithmetic, per_device(): jnp.where((position < prompt_length[0])[:, None, None], prompt_kv, jnp.ze...  20.4 us
    all_to_all x1, local copies, waits for them, and re-layouts, per_device(): lax.all_to_all(kept, 'seq', split_axis=1, concat_axis=0, tiled=True)  18.6 us
    all_gather x3, blocking collectives, merged(): gathered = jax.tree.map(lambda a: lax.all_gather(a, axis), part)  16.8 us
    dot_general x1, matrix products, per_device(): jnp.einsum('rgd,rpd->rgp', query_rows, k_cache, preferred_element_type=jn...  10.3 us
  transfers between devices with their start and end apart: 1, of which 1 were waited for; matrix products, arithmetic and copies ran while one was open for 6% of the time, Pallas kernels for 0%

commit v1 on v0

--- a/solution.py
+++ b/solution.py
@@ -34,7 +34,15 @@
     kept = jnp.where(
         (position < prompt_length[0])[:, None, None], prompt_kv, jnp.zeros_like(prompt_kv)
     )
-    prompt_owned = lax.all_to_all(kept, "seq", split_axis=1, concat_axis=0, tiled=True)
+    ways, here = (lax.axis_size("seq"), lax.axis_index("seq"))
+    width_2 = kept.shape[1] // ways
+    turned = jnp.roll(kept, -here * width_2, axis=1)
+    got = [lax.slice_in_dim(turned, 0, width_2, axis=1)]
+    for far in range(1, ways):
+        sent = lax.slice_in_dim(turned, far * width_2, (far + 1) * width_2, axis=1)
+        got.append(lax.ppermute(sent, "seq", [(d, (d + far) % ways) for d in range(ways)]))
+    line = jnp.concatenate(got[::-1], axis=0)
+    prompt_owned = jnp.roll(line, (here + 1) * got[0].shape[0], axis=0)
     resident = lengths.shape[0]
     pair_rows = k_cache.shape[0]
     span = k_cache.shape[1]

time: 413 us -> 454 us (1.099)
  local copies, waits for them, and re-layouts: 22.3 us -> 68.8 us
  waiting for transfers between devices: 324 us -> 315 us
  other arithmetic: 22.3 us -> 28.8 us
    all_to_all x1 -> x0, waiting for transfers between devices: 324 us -> none  [per_device(): lax.all_to_all(kept, 'seq', split_axis=1, concat_axis=0, tiled=True)]
    ppermute x0 -> x3, waiting for transfers between devices: none -> 315 us  [per_device(): lax.ppermute(sent, 'seq', [(d, (d + far) % ways) for d in range(ways)])]
    unnamed x9 -> x18, local copies, waits for them, and re-layouts: 0.63 us -> 40.8 us
    all_to_all x1 -> x0, local copies, waits for them, and re-layouts: 18.6 us -> none  [per_device(): lax.all_to_all(kept, 'seq', split_axis=1, concat_axis=0, tiled=True)]
    dynamic_slice x0 -> x1, local copies, waits for them, and re-layouts: none -> 14.5 us  [per_device(): prompt_owned = jnp.roll(line, (here + 1) * got[0].shape[0], axis=0)]
    concatenate x0 -> x1, other arithmetic: none -> 11.8 us  [per_device(): turned = jnp.roll(kept, -here * width_2, axis=1)]
    all_to_all x1 -> x0, starting transfers between devices: 7.11 us -> none  [per_device(): lax.all_to_all(kept, 'seq', split_axis=1, concat_axis=0, tiled=True)]
    ppermute x0 -> x3, starting transfers between devices: none -> 5.94 us  [per_device(): lax.ppermute(sent, 'seq', [(d, (d + far) % ways) for d in range(ways)])]
  transfers between devices with their start and end apart: 1 -> 3, of which waited for: 1 -> 2; matrix products, arithmetic and copies ran while one was open for 6% -> 7% of each run, Pallas kernels for 0% -> 0%
where the time goes in v1:
time: 454 us; the launch traced here: 453 us
  waiting for transfers between devices  315 us (69%)
  local copies, waits for them, and re-layouts  68.8 us (15%)
  other arithmetic  28.8 us (6%)
  matrix products  17.5 us (4%)
  blocking collectives  15.7 us (3%)
  starting transfers between devices  5.94 us (1%)
    ppermute x3, waiting for transfers between devices, per_device(): lax.ppermute(sent, 'seq', [(d, (d + far) % ways) for d in range(ways)])  315 us
    unnamed x18, local copies, waits for them, and re-layouts  40.8 us
    all_gather x3, blocking collectives, merged(): gathered = jax.tree.map(lambda a: lax.all_gather(a, axis), part)  15.7 us
    select_n x1, other arithmetic, per_device(): jnp.where((position < prompt_length[0])[:, None, None], prompt_kv, jnp.ze...  15 us
    dynamic_slice x1, local copies, waits for them, and re-layouts, per_device(): prompt_owned = jnp.roll(line, (here + 1) * got[0].shape[0], axis=0)  14.5 us
    concatenate x1, other arithmetic, per_device(): turned = jnp.roll(kept, -here * width_2, axis=1)  11.8 us
    dot_general x1, matrix products, per_device(): jnp.einsum('rgd,rpd->rgp', query_rows, k_cache, preferred_element_type=jn...  10.3 us
  transfers between devices with their start and end apart: 3, of which 2 were waited for; matrix products, arithmetic and copies ran while one was open for 7% of the time, Pallas kernels for 0%

profile of v1, /device:TPU:0, one launch (start us, length us, event | category | flops | bytes accessed | tf_op | source)
XLA Modules:
  0.0 453.0 jit_solution(11773508913194874765)
XLA Ops:
  1.4 15.0 %broadcast_select_fusion = bf16[1024,64,128]{2,1,0:T(8,128)(2,1)} fusion(bf16[1024,64,128]{2,1,0:T(8,128)(2,1)} %param.10, pred[1024]{0:T(1024)(128)(4,1)S(1)} %add_compare_fusion), kind=kLoop, calls=%fused_computation.15 | loop fusion | flops 8388608 | bytes 33555456 | tf_op jit(solution)/shard_map/jit(_where)/select_n | solution.py:34
  16.4 11.8 %fusion.3 = bf16[1024,64,128]{2,1,0:T(8,128)(2,1)S(1)} fusion(s32[]{:T(128)S(6)} %select_n.102, bf16[1024,64,128]{2,1,0:T(8,128)(2,1)} %broadcast_select_fusion), kind=kLoop, calls=%fused_computation.14 | loop fusion | flops 33554432 | bytes 33554436 | tf_op jit(solution)/shard_map/jit(_roll_dynamic)/concatenate | solution.py:39
  28.2 6.2 %copy-done.2 = bf16[1024,64,128]{2,1,0:T(8,128)(2,1)} copy-done((bf16[1024,64,128]{2,1,0:T(8,128)(2,1)}, bf16[1024,64,128]{2,1,0:T(8,128)(2,1)S(1)}, u32[]{:S(2)}) %copy-start.2) | copy-done | bytes 16777240
  34.4 5.5 %fusion.22 = (bf16[1024,16,128]{2,1,0:T(8,128)(2,1)}, bf16[1024,16,128]{2,1,0:T(8,128)(2,1)}, bf16[1024,16,128]{2,1,0:T(8,128)(2,1)}) fusion(bf16[1024,64,128]{2,1,0:T(8,128)(2,1)S(1)} %fusion.3), kind=kLoop, calls=%fused_computation.66 | loop fusion | bytes 25165824 | tf_op jit(solution)/shard_map/slice | solution.py:42
  39.9 5.0 %collective-permute-start = (bf16[1024,16,128]{2,1,0:T(8,128)(2,1)}, bf16[1024,16,128]{2,1,0:T(8,128)(2,1)}, u32[]{:S(2)}, u32[]{:S(2)}) collective-permute-start(bf16[1024,16,128]{2,1,0:T(8,128)(2,1)} %get-tuple-element.206), channel_id=1, source_target_pairs={{0,12},{4,0},{8,4},{12,8},{1,13},{5,1},{9,5},{13,9},{2,14},{6,2},{... | collective-permute-start | bytes 12582920 | tf_op jit(solution)/shard_map/ppermute | solution.py:43
  44.8 1.0 collective-permute-start.2
  47.5 10.3 %fusion.23 = (f32[32,2]{1,0:T(8,128)S(1)}, f32[32,2,2048]{2,1,0:T(2,128)S(1)}) fusion(bf16[32,2,128]{2,1,0:T(2,128)(2,1)S(1)} %gather_fusion.1, bf16[32,2048,128]{2,1,0:T(8,128)(2,1)} %param.14, pred[32,2048]{1,0:T(8,128)(4,1)S(1)} %broadcast_compare_fusion), kind=kOutput, calls=%fused_computation.67 | convolution fusion | flops 33947584 | bytes 17383680 | tf_op jit(solution)/shard_map/rgd,rpd->rgp/dot_general | solution.py:64
  57.9 7.1 %fusion.5 = f32[32,2,128]{2,1,0:T(2,128)S(1)} fusion(bf16[32,2048,128]{2,1,0:T(8,128)(2,1)} %param.15, f32[32,2,2048]{2,1,0:T(2,128)S(1)} %get-tuple-element.210, pred[32,2048]{1,0:T(8,128)(4,1)S(1)} %broadcast_compare_fusion, f32[32,2]{1,0:T(8,128)S(1)} %get-tuple-element.209), kind=kOutput, calls=%fused_computation.21 | convolution fusion | flops 33947648 | bytes 17400064 | tf_op jit(solution)/shard_map/rgp,rpd->rgd/dot_general | solution.py:76
  65.0 5.4 %all-gather.2 = f32[128,2,128]{2,1,0:T(2,128)S(1)} all-gather(f32[32,2,128]{2,1,0:T(2,128)S(1)} %fusion.5), channel_id=4, replica_groups=mesh['groups'=2,'seq'=4,'tp'=4] {'tp'}, dimensions={0}, use_global_device_ids=true | all-gather | bytes 163840 | tf_op jit(solution)/shard_map/all_gather | solution.py:11
  70.4 0.7 fusion.7
  72.1 5.1 %all-gather.4 = f32[4,32,2]{1,2,0:T(2,128)S(1)} all-gather(f32[1,32,2]{1,2,0:T(2,128)S(1)} %bitcast.63), channel_id=3, replica_groups=mesh['groups'=2,'seq'=4,'tp'=4] {'tp'}, dimensions={0}, use_global_device_ids=true | all-gather | bytes 1280 | tf_op jit(solution)/shard_map/all_gather | solution.py:11
  77.1 5.2 %all-gather.3 = f32[4,32,2]{1,2,0:T(2,128)S(1)} all-gather(f32[1,32,2]{1,2,0:T(2,128)S(1)} %bitcast.62), channel_id=2, replica_groups=mesh['groups'=2,'seq'=4,'tp'=4] {'tp'}, dimensions={0}, use_global_device_ids=true | all-gather | bytes 1280 | tf_op jit(solution)/shard_map/all_gather | solution.py:11
  82.4 1.3 while.19
  84.8 51.4 %collective-permute-done = bf16[1024,16,128]{2,1,0:T(8,128)(2,1)} collective-permute-done((bf16[1024,16,128]{2,1,0:T(8,128)(2,1)}, bf16[1024,16,128]{2,1,0:T(8,128)(2,1)}, u32[]{:S(2)}, u32[]{:S(2)}) %collective-permute-start) | collective-permute-done | bytes 4194336 | tf_op jit(solution)/shard_map/ppermute | solution.py:43
  136.2 4.8 %constant_dynamic-update-slice_fusion.5 = bf16[8192,16,128]{2,1,0:T(8,128)(2,1)} fusion(bf16[1024,16,128]{2,1,0:T(8,128)(2,1)} %collective-permute-done), kind=kLoop, calls=%fused_computation.35 | loop fusion | bytes 8388608
  141.0 263.4 %collective-permute-done.1 = bf16[1024,16,128]{2,1,0:T(8,128)(2,1)} collective-permute-done((bf16[1024,16,128]{2,1,0:T(8,128)(2,1)}, bf16[1024,16,128]{2,1,0:T(8,128)(2,1)}, u32[]{:S(2)}, u32[]{:S(2)}) %collective-permute-start.1) | collective-permute-done | bytes 4194336 | tf_op jit(solution)/shard_map/ppermute | solution.py:43
  404.4 4.9 %constant_dynamic-update-slice_fusion.4 = bf16[8192,16,128]{2,1,0:T(8,128)(2,1)} fusion(bf16[8192,16,128]{2,1,0:T(8,128)(2,1)} %constant_dynamic-update-slice_fusion.5, bf16[1024,16,128]{2,1,0:T(8,128)(2,1)} %collective-permute-done.1), kind=kLoop, calls=%fused_computation.34 | loop fusion | bytes 8388608
  409.3 4.9 %constant_dynamic-update-slice_fusion.3 = bf16[8192,16,128]{2,1,0:T(8,128)(2,1)} fusion(bf16[8192,16,128]{2,1,0:T(8,128)(2,1)} %constant_dynamic-update-slice_fusion.4, bf16[1024,16,128]{2,1,0:T(8,128)(2,1)} %collective-permute-done.2), kind=kLoop, calls=%fused_computation.33 | loop fusion | bytes 8388608
  414.1 4.9 %slice_dynamic-update-slice_fusion = bf16[8192,16,128]{2,1,0:T(8,128)(2,1)} fusion(bf16[8192,16,128]{2,1,0:T(8,128)(2,1)} %constant_dynamic-update-slice_fusion.3, bf16[1024,64,128]{2,1,0:T(8,128)(2,1)} %copy-done.2), kind=kLoop, calls=%fused_computation.16 | loop fusion | bytes 8388608
  419.0 4.8 %constant_dynamic-update-slice_fusion.2 = bf16[8192,16,128]{2,1,0:T(8,128)(2,1)} fusion(bf16[8192,16,128]{2,1,0:T(8,128)(2,1)} %slice_dynamic-update-slice_fusion, bf16[1024,16,128]{2,1,0:T(8,128)(2,1)} %collective-permute-done), kind=kLoop, calls=%fused_computation.32 | loop fusion | bytes 8388608
  423.8 4.9 %constant_dynamic-update-slice_fusion.1 = bf16[8192,16,128]{2,1,0:T(8,128)(2,1)} fusion(bf16[8192,16,128]{2,1,0:T(8,128)(2,1)} %constant_dynamic-update-slice_fusion.2, bf16[1024,16,128]{2,1,0:T(8,128)(2,1)} %collective-permute-done.1), kind=kLoop, calls=%fused_computation.31 | loop fusion | bytes 8388608
  428.7 4.9 %constant_dynamic-update-slice_fusion = bf16[8192,16,128]{2,1,0:T(8,128)(2,1)} fusion(bf16[8192,16,128]{2,1,0:T(8,128)(2,1)} %constant_dynamic-update-slice_fusion.1, bf16[1024,16,128]{2,1,0:T(8,128)(2,1)} %collective-permute-done.2), kind=kLoop, calls=%fused_computation.30 | loop fusion | bytes 8388608
  433.6 4.9 %slice_dynamic-update-slice_fusion.1 = bf16[8192,16,128]{2,1,0:T(8,128)(2,1)} fusion(bf16[8192,16,128]{2,1,0:T(8,128)(2,1)} %constant_dynamic-update-slice_fusion, bf16[1024,64,128]{2,1,0:T(8,128)(2,1)} %copy-done.2), kind=kLoop, calls=%fused_computation.17 | loop fusion | bytes 8388608 | tf_op jit(solution)/shard_map/jit(_roll_dynamic)/concatenate | solution.py:45
  438.5 14.5 %constant_dynamic-slice_fusion.1 = bf16[4096,16,128]{2,1,0:T(8,128)(2,1)} fusion(bf16[8192,16,128]{2,1,0:T(8,128)(2,1)} %slice_dynamic-update-slice_fusion.1, s32[]{:T(128)S(6)} %select_n.104), kind=kLoop, calls=%fused_computation.58 | loop fusion | bytes 33554436 | tf_op jit(solution)/shard_map/jit(_roll_dynamic)/dynamic_slice | solution.py:45
  (48 shorter events, 5.1 us)
Async XLA Ops:
  0.6 70.5 %copy-start = (bf16[8,16,2,128]{3,2,1,0:T(2,128)(2,1)S(1)}, bf16[8,16,2,128]{3,2,1,0:T(2,128)(2,1)}, u32[]{:S(2)}) copy-start(bf16[8,16,2,128]{3,2,1,0:T(2,128)(2,1)} %param.13) | copy-start | bytes 196612
  28.2 6.2 %copy-start.2 = (bf16[1024,64,128]{2,1,0:T(8,128)(2,1)}, bf16[1024,64,128]{2,1,0:T(8,128)(2,1)S(1)}, u32[]{:S(2)}) copy-start(bf16[1024,64,128]{2,1,0:T(8,128)(2,1)S(1)} %fusion.3) | copy-start | bytes 50331652
  34.4 11.4 %copy-start.4 = (s32[8]{0:T(128)S(1)}, s32[8]{0:T(128)}, u32[]{:S(2)}) copy-start(s32[8]{0:T(128)} %param.17) | copy-start | bytes 100
  34.4 11.6 %copy-start.3 = (bf16[8,4096]{1,0:T(8,128)(2,1)S(1)}, bf16[8,4096]{1,0:T(8,128)(2,1)}, u32[]{:S(2)}) copy-start(bf16[8,4096]{1,0:T(8,128)(2,1)} %param.12) | copy-start | bytes 196612
  34.4 11.6 %copy-start.1 = (s32[8]{0:T(128)S(1)}, s32[8]{0:T(128)}, u32[]{:S(2)}) copy-start(s32[8]{0:T(128)} %param.16) | copy-start | bytes 100
  39.9 96.3 %collective-permute-start = (bf16[1024,16,128]{2,1,0:T(8,128)(2,1)}, bf16[1024,16,128]{2,1,0:T(8,128)(2,1)}, u32[]{:S(2)}, u32[]{:S(2)}) collective-permute-start(bf16[1024,16,128]{2,1,0:T(8,128)(2,1)} %get-tuple-element.206), channel_id=1, source_target_pairs={{0,12},{4,0},{8,4},{12,8},{1,13},{5,1},{9,5},{13,9},{2,14},{6,2},{... | collective-permute-start | bytes 12582920 | tf_op jit(solution)/shard_map/ppermute | solution.py:43
  44.8 359.5 %collective-permute-start.1 = (bf16[1024,16,128]{2,1,0:T(8,128)(2,1)}, bf16[1024,16,128]{2,1,0:T(8,128)(2,1)}, u32[]{:S(2)}, u32[]{:S(2)}) collective-permute-start(bf16[1024,16,128]{2,1,0:T(8,128)(2,1)} %get-tuple-element.205), channel_id=1, source_target_pairs={{0,8},{4,12},{8,0},{12,4},{1,9},{5,13},{9,1},{13,5},{2,10},{6,14},... | collective-permute-start | bytes 12582920 | tf_op jit(solution)/shard_map/ppermute | solution.py:43
  44.8 364.4 %collective-permute-start.2 = (bf16[1024,16,128]{2,1,0:T(8,128)(2,1)}, bf16[1024,16,128]{2,1,0:T(8,128)(2,1)}, u32[]{:S(2)}, u32[]{:S(2)}) collective-permute-start(bf16[1024,16,128]{2,1,0:T(8,128)(2,1)} %get-tuple-element.204), channel_id=1, source_target_pairs={{0,4},{4,8},{8,12},{12,0},{1,5},{5,9},{9,13},{13,1},{2,6},{6,10},{... | collective-permute-start | bytes 12582920 | tf_op jit(solution)/shard_map/ppermute | solution.py:43
